TPU v7x, 32 devices: a whole 2x2x4 slice. The times are simulated.
32 devices in a mesh: groups: 2 (over x), steps: 16 (over z, y, core).
Axes of the slice: x: 2, y: 2, z: 4, core: 2. Of those that a mesh axis runs over, the one named last changes fastest.
Arguments:
- states: float32 [32, 4, 4096], P(('groups', 'steps')), parts along dimension 0, may hold values from -6 to 6
- t_sched: int32 [66], P('groups'), parts along dimension 0, may hold values from 0 to 999, as said below
- advances: int32 [4], P('groups'), parts along dimension 0, may hold values from 1 to 16, as said below
- in_weight: bfloat16 [320, 4], replicated, may hold values from -3 to 3
- time_weight: float32 [320, 320], replicated, may hold values from -0.3125 to 0.3125
- mid_weight: bfloat16 [320, 320], replicated, may hold values from -0.3125 to 0.3125
- out_weight: bfloat16 [4, 320], replicated, may hold values from -0.3125 to 0.3125
Outputs:
- final_states: float32 [32, 4, 4096], P(('groups', 'steps')), parts along dimension 0
- errors: float32 [4, 4, 16], P('groups', None, 'steps'), parts along dimension 0
There are 2 independent parts, one for each index of `groups`. A program takes and returns all parts, laid end to end along the dimension named above; an argument that names none is the same for every part. Nothing has to cross between parts.
Inputs may be any that keep to these rules, and one draw needn't show every extreme that they name: `t_sched`: strictly decreasing. Some round advances by exactly 16.
All inputs are finite; a program needn't handle non-finite values.
Results may differ from a plain program's by a relative error of at most 0.0024.
Values sent between devices are 32-bit elements; how exact they have to be, the bound alone decides.
A program may use at most 64 MiB of HBM per device.

v0:
```python
import math

import jax
import jax.numpy as jnp
from jax import lax
from jax.sharding import PartitionSpec as P

TSTEPS = 1000
ITERS = 4
ROUNDS = 2


def entering(part, axis, combine, identity):
    place = lax.axis_index(axis)
    gathered = lax.all_gather(part, axis)
    state = jnp.zeros_like(part) + jnp.asarray(identity, part.dtype)

    def one(hop, state):
        return combine(state, lax.dynamic_index_in_dim(gathered, hop, 0, False))

    return lax.fori_loop(0, place, one, state)


def from_behind(value, axis, by):
    devices = lax.axis_size(axis)
    pairs = [(i, i + by) for i in range(devices) if 0 <= i + by < devices]
    return lax.ppermute(value, axis, pairs)


def from_root(block, axis, source):
    block = jnp.where(lax.axis_index(axis) == source, block, jnp.zeros_like(block))
    return lax.psum(block, axis)


def alpha_table():
    levels = jnp.arange(TSTEPS, dtype=jnp.float32)
    low = math.sqrt(0.00085)
    high = math.sqrt(0.012)
    betas = (low + (high - low) * levels / (TSTEPS - 1)) ** 2
    return jnp.exp(jnp.cumsum(jnp.log1p(-betas)))


def time_features(stamp, width):
    halfwidth = width // 2
    freqs = jnp.exp(-math.log(10000.0) * jnp.arange(halfwidth, dtype=jnp.float32) / halfwidth)
    angles = stamp.astype(jnp.float32) * freqs
    return jnp.concatenate([jnp.cos(angles), jnp.sin(angles)])


def lookup(alphas, stamp):
    levels = jnp.arange(alphas.shape[0], dtype=jnp.int32)
    return jnp.sum(jnp.where(levels == stamp, alphas, 0.0))


def denoise(state, embed, in_weight, mid_weight, out_weight):
    pre = (
        jnp.dot(in_weight, state.astype(jnp.bfloat16), preferred_element_type=jnp.float32)
        + embed[:, None]
    )
    hidden_one = jax.nn.silu(pre).astype(jnp.bfloat16)
    mixed = jnp.dot(mid_weight, hidden_one, preferred_element_type=jnp.float32)
    hidden_two = (jax.nn.silu(mixed) + pre).astype(jnp.bfloat16)
    return jnp.dot(out_weight, hidden_two, preferred_element_type=jnp.float32)


def add_terms(earlier, later):
    return earlier + later


def shards(states, t_sched, advances, in_weight, time_weight, mid_weight, out_weight):
    window = lax.axis_size("steps")
    own_index = lax.axis_index("steps")
    alphas = alpha_table()
    current = states
    window_start = jnp.int32(0)
    error_rows = []
    for round_no in range(ROUNDS):
        stamp_now = lax.dynamic_slice_in_dim(t_sched, window_start + own_index, 1)[0]
        stamp_next = lax.dynamic_slice_in_dim(t_sched, window_start + own_index + 1, 1)[0]
        alpha_now = lookup(alphas, stamp_now)
        alpha_next = lookup(alphas, stamp_next)
        coef_one = jnp.sqrt(alpha_next / alpha_now)
        coef_two = jnp.sqrt(1.0 - alpha_next) - coef_one * jnp.sqrt(1.0 - alpha_now)
        feats = time_features(stamp_now, time_weight.shape[1])
        embed = jnp.dot(time_weight, feats, precision=lax.Precision.HIGHEST)
        is_first = own_index == 0
        sweep_rows = []
        for sweep in range(ITERS):
            noise = denoise(current[0], embed, in_weight, mid_weight, out_weight)
            drift = (coef_one - 1.0) * current + coef_two * noise[None]
            term = drift + jnp.where(is_first, current, 0.0)
            prefix = entering(term, "steps", add_terms, jnp.zeros_like(term))
            updated = jnp.where(is_first, current, prefix)
            sweep_rows.append(jnp.mean((updated - current) ** 2))
            current = updated
        error_rows.append(jnp.stack(sweep_rows))
        advance = advances[round_no]
        target = own_index + advance
        moved = current
        bit_count = (window - 1).bit_length()
        for bit_no in reversed(range(bit_count)):
            shifted = from_behind(moved, "steps", -(1 << bit_no))
            moved = jnp.where(advance >> bit_no & 1 == 1, shifted, moved)
        last_state = from_root(current, "steps", window - 1)
        current = jnp.where(target > window - 1, last_state, moved)
        window_start = window_start + advance
    errors = jnp.stack(error_rows).reshape(ROUNDS, ITERS, 1)
    return (current, errors)


def solution(mesh):
    in_specs = (P(("groups", "steps"), None, None), P("groups"), P("groups"), P(), P(), P(), P())
    out_specs = (P(("groups", "steps"), None, None), P("groups", None, "steps"))
    return jax.shard_map(shards, mesh=mesh, in_specs=in_specs, out_specs=out_specs, check_vma=False)
```

profile of v0, /device:TPU:10, one launch (start us, length us, event | category | flops | bytes accessed | tf_op | source)
XLA Modules:
  0.0 730.7 jit_solution(1831922749544602401)
XLA Ops:
  18.5 4.1 convolution_add_fusion.7
  22.7 8.2 %fusion.24 = f32[1,4,4096]{2,1,0:T(4,128)} fusion(bf16[4,320]{1,0:T(4,128)(2,1)S(1)} %copy-done.4, f32[320,4096]{1,0:T(8,128)} %convolution_add_fusion.7, bf16[320,320]{1,0:T(8,128)(2,1)S(1)} %copy-done.3, f32[1,4,4096]{2,1,0:T(4,128)S(1)} %copy-done.1, f32[]{:T(128)S(6)} %sub.57, f32[]{:T(128)S(6)} %sub.54, pred[]{:T(512)S(6)} %eq.57), kind=kOutput, calls=%fused_computation.72 | convolution fusion | flops 863846400 | bytes 5581321 | tf_op jit(solution)/shard_map/dot_general | solution.py:63
  31.0 38.1 %all-gather.17.cloned.1.call-done = f32[16,4,4096]{2,1,0:T(4,128)} async-done(((f32[1,4,4096]{2,1,0:T(4,128)}), f32[16,4,4096]{2,1,0:T(4,128)}) %all-gather.17.cloned.1.call-update) | async-done | bytes 1048592 | tf_op jit(solution)/shard_map/all_gather | solution.py:15
  69.1 3.6 while.80
  75.9 8.2 %fusion.21 = f32[1,4,4096]{2,1,0:T(4,128)} fusion(bf16[4,320]{1,0:T(4,128)(2,1)S(1)} %copy-done.4, f32[320,4096]{1,0:T(8,128)} %fusion.6, bf16[320,320]{1,0:T(8,128)(2,1)S(1)} %copy-done.3, f32[1,4,4096]{2,1,0:T(4,128)S(1)} %broadcast_select_fusion.15, f32[]{:T(128)S(6)} %sub.57, f32[]{:T(128)S(6)} %sub.54, pred[]{:T(512)S(6)} %eq.57), kind=kOutput, calls=%fused_computation.68 | convolution fusion | flops 863846400 | bytes 5581321 | tf_op jit(solution)/shard_map/dot_general | solution.py:63
  84.1 46.6 %all-gather.19.cloned.1.call-done = f32[16,4,4096]{2,1,0:T(4,128)} async-done(((f32[1,4,4096]{2,1,0:T(4,128)}), f32[16,4,4096]{2,1,0:T(4,128)}) %all-gather.19.cloned.1.call-update) | async-done | bytes 1048592 | tf_op jit(solution)/shard_map/all_gather | solution.py:15
  130.8 3.8 while.81
  137.8 8.2 %fusion.18 = f32[1,4,4096]{2,1,0:T(4,128)} fusion(bf16[4,320]{1,0:T(4,128)(2,1)S(1)} %copy-done.4, f32[320,4096]{1,0:T(8,128)} %fusion.5, bf16[320,320]{1,0:T(8,128)(2,1)S(1)} %copy-done.3, f32[1,4,4096]{2,1,0:T(4,128)S(1)} %broadcast_select_fusion.14, f32[]{:T(128)S(6)} %sub.57, f32[]{:T(128)S(6)} %sub.54, pred[]{:T(512)S(6)} %eq.57), kind=kOutput, calls=%fused_computation.64 | convolution fusion | flops 863846400 | bytes 5581321 | tf_op jit(solution)/shard_map/dot_general | solution.py:63
  146.1 46.6 %all-gather.21.cloned.1.call-done = f32[16,4,4096]{2,1,0:T(4,128)} async-done(((f32[1,4,4096]{2,1,0:T(4,128)}), f32[16,4,4096]{2,1,0:T(4,128)}) %all-gather.21.cloned.1.call-update) | async-done | bytes 1048592 | tf_op jit(solution)/shard_map/all_gather | solution.py:15
  192.7 3.6 while.82
  199.5 8.1 %fusion.15 = f32[1,4,4096]{2,1,0:T(4,128)} fusion(bf16[4,320]{1,0:T(4,128)(2,1)S(1)} %copy-done.4, f32[320,4096]{1,0:T(8,128)} %fusion.4, bf16[320,320]{1,0:T(8,128)(2,1)S(1)} %copy-done.3, f32[1,4,4096]{2,1,0:T(4,128)S(1)} %broadcast_select_fusion.13, f32[]{:T(128)S(6)} %sub.57, f32[]{:T(128)S(6)} %sub.54, pred[]{:T(512)S(6)} %eq.57), kind=kOutput, calls=%fused_computation.60 | convolution fusion | flops 863846400 | bytes 5581321 | tf_op jit(solution)/shard_map/dot_general | solution.py:63
  207.7 46.6 %all-gather.23.cloned.1.call-done = f32[16,4,4096]{2,1,0:T(4,128)} async-done(((f32[1,4,4096]{2,1,0:T(4,128)}), f32[16,4,4096]{2,1,0:T(4,128)}) %all-gather.23.cloned.1.call-update) | async-done | bytes 1048592 | tf_op jit(solution)/shard_map/all_gather | solution.py:15
  254.4 3.6 while.83
  262.7 9.4 %collective-permute-done = f32[1,4,4096]{2,1,0:T(4,128)S(1)} collective-permute-done((f32[1,4,4096]{2,1,0:T(4,128)S(1)}, f32[1,4,4096]{2,1,0:T(4,128)S(1)}, u32[]{:S(2)}, u32[]{:S(2)}) %collective-permute-start) | collective-permute-done | bytes 65568 | tf_op jit(solution)/shard_map/ppermute | solution.py:27
  274.7 4.2 collective-permute-done.1
  278.9 4.0 collective-permute-start.2
  292.5 78.7 %all-reduce.4.cloned.1.call-done = f32[1,4,4096]{2,1,0:T(4,128)} async-done(((f32[1,4,4096]{2,1,0:T(4,128)}), f32[1,4,4096]{2,1,0:T(4,128)}) %all-reduce.4.cloned.1.call-update) | async-done | bytes 65552 | tf_op jit(solution)/shard_map/psum | solution.py:32
  375.3 8.2 %select_add_fusion.2 = f32[1,4,4096]{2,1,0:T(4,128)} fusion(f32[1,4,4096]{2,1,0:T(4,128)S(1)} %select_select_fusion.1, bf16[4,320]{1,0:T(4,128)(2,1)S(1)} %copy-done.4, f32[320,4096]{1,0:T(8,128)} %fusion.3, bf16[320,320]{1,0:T(8,128)(2,1)S(1)} %copy-done.3, f32[]{:T(128)S(6)} %sub.61, f32[]{:T(128)S(6)} %sub.58, pred[]{:T(512)S(6)} %eq.57), kind=kOutput, calls=%fused_computation.94 | convolution fusion | flops 863846400 | bytes 5581321 | tf_op jit(solution)/shard_map/dot_general | solution.py:63
  383.5 36.0 %all-gather.25.cloned.1.call-done = f32[16,4,4096]{2,1,0:T(4,128)} async-done(((f32[1,4,4096]{2,1,0:T(4,128)}), f32[16,4,4096]{2,1,0:T(4,128)}) %all-gather.25.cloned.1.call-update) | async-done | bytes 1048592 | tf_op jit(solution)/shard_map/all_gather | solution.py:15
  419.5 3.6 while.84
  426.3 8.2 %select_add_fusion.1 = f32[1,4,4096]{2,1,0:T(4,128)} fusion(f32[1,4,4096]{2,1,0:T(4,128)S(1)} %broadcast_select_fusion.11, bf16[4,320]{1,0:T(4,128)(2,1)S(1)} %copy-done.4, f32[320,4096]{1,0:T(8,128)} %fusion.2, bf16[320,320]{1,0:T(8,128)(2,1)S(1)} %copy-done.3, f32[]{:T(128)S(6)} %sub.61, f32[]{:T(128)S(6)} %sub.58, pred[]{:T(512)S(6)} %eq.57), kind=kOutput, calls=%fused_computation.93 | convolution fusion | flops 863846400 | bytes 5581321 | tf_op jit(solution)/shard_map/dot_general | solution.py:63
  434.6 46.6 %all-gather.27.cloned.1.call-done = f32[16,4,4096]{2,1,0:T(4,128)} async-done(((f32[1,4,4096]{2,1,0:T(4,128)}), f32[16,4,4096]{2,1,0:T(4,128)}) %all-gather.27.cloned.1.call-update) | async-done | bytes 1048592 | tf_op jit(solution)/shard_map/all_gather | solution.py:15
  481.2 3.8 while.85
  488.2 8.2 %select_add_fusion = f32[1,4,4096]{2,1,0:T(4,128)} fusion(f32[1,4,4096]{2,1,0:T(4,128)S(1)} %broadcast_select_fusion.10, bf16[4,320]{1,0:T(4,128)(2,1)S(1)} %copy-done.4, f32[320,4096]{1,0:T(8,128)} %fusion.1, bf16[320,320]{1,0:T(8,128)(2,1)S(1)} %copy-done.3, f32[]{:T(128)S(6)} %sub.61, f32[]{:T(128)S(6)} %sub.58, pred[]{:T(512)S(6)} %eq.57), kind=kOutput, calls=%fused_computation.92 | convolution fusion | flops 863846400 | bytes 5581321 | tf_op jit(solution)/shard_map/dot_general | solution.py:63
  496.4 46.6 %all-gather.29.cloned.1.call-done = f32[16,4,4096]{2,1,0:T(4,128)} async-done(((f32[1,4,4096]{2,1,0:T(4,128)}), f32[16,4,4096]{2,1,0:T(4,128)}) %all-gather.29.cloned.1.call-update) | async-done | bytes 1048592 | tf_op jit(solution)/shard_map/all_gather | solution.py:15
  543.0 3.6 while.86
  549.8 8.1 %fusion.9 = f32[1,4,4096]{2,1,0:T(4,128)} fusion(bf16[4,320]{1,0:T(4,128)(2,1)S(1)} %copy-done.4, f32[320,4096]{1,0:T(8,128)} %fusion, bf16[320,320]{1,0:T(8,128)(2,1)S(1)} %copy-done.3, f32[1,4,4096]{2,1,0:T(4,128)S(1)} %broadcast_select_fusion.9, f32[]{:T(128)S(6)} %sub.61, f32[]{:T(128)S(6)} %sub.58, pred[]{:T(512)S(6)} %eq.57), kind=kOutput, calls=%fused_computation.50 | convolution fusion | flops 863846400 | bytes 5581321 | tf_op jit(solution)/shard_map/dot_general | solution.py:63
  558.1 46.6 %all-gather.31.cloned.1.call-done = f32[16,4,4096]{2,1,0:T(4,128)} async-done(((f32[1,4,4096]{2,1,0:T(4,128)}), f32[16,4,4096]{2,1,0:T(4,128)}) %all-gather.31.cloned.1.call-update) | async-done | bytes 1048592 | tf_op jit(solution)/shard_map/all_gather | solution.py:15
  604.7 3.6 while.87
  615.9 6.4 collective-permute-done.4
  629.2 4.0 collective-permute-start.6
  638.9 83.3 %all-reduce.6.cloned.1.call-done = f32[1,4,4096]{2,1,0:T(4,128)} async-done(((f32[1,4,4096]{2,1,0:T(4,128)}), f32[1,4,4096]{2,1,0:T(4,128)}) %all-reduce.6.cloned.1.call-update) | async-done | bytes 65552 | tf_op jit(solution)/shard_map/psum | solution.py:32
  (125 shorter events, 83.3 us)
Async XLA Ops:
  7.2 10.8 %copy-start = (f32[320,320]{1,0:T(8,128)S(1)}, f32[320,320]{1,0:T(8,128)}, u32[]{:S(2)}) copy-start(f32[320,320]{1,0:T(8,128)} %param.27) | copy-start | bytes 1228804
  7.2 15.5 %copy-start.1 = (f32[1,4,4096]{2,1,0:T(4,128)S(1)}, f32[1,4,4096]{2,1,0:T(4,128)}, u32[]{:S(2)}) copy-start(f32[1,4,4096]{2,1,0:T(4,128)} %param.23) | copy-start | bytes 196612
  7.2 15.5 %copy-start.3 = (bf16[320,320]{1,0:T(8,128)(2,1)S(1)}, bf16[320,320]{1,0:T(8,128)(2,1)}, u32[]{:S(2)}) copy-start(bf16[320,320]{1,0:T(8,128)(2,1)} %param.28) | copy-start | bytes 614404
  7.2 15.5 %copy-start.4 = (bf16[4,320]{1,0:T(4,128)(2,1)S(1)}, bf16[4,320]{1,0:T(4,128)(2,1)}, u32[]{:S(2)}) copy-start(bf16[4,320]{1,0:T(4,128)(2,1)} %param.29) | copy-start | bytes 7684
  7.2 61.8 %all-gather.17.cloned.1.call-start = ((), (), s32[]{:S(2)}) async-start(), calls=%async_computation.2 | async-start | bytes 1114112 | tf_op jit(solution)/shard_map/all_gather | solution.py:15
  22.7 50.0 %copy-start.2 = (bf16[320,4]{0,1:T(4,128)(2,1)S(1)}, bf16[320,4]{0,1:T(4,128)(2,1)}, u32[]{:S(2)}) copy-start(bf16[320,4]{0,1:T(4,128)(2,1)} %param.26) | copy-start | bytes 7684
  30.9 99.9 %all-gather.19.cloned.1.call-start = ((), (), s32[]{:S(2)}) async-start(), calls=%async_computation.3 | async-start | bytes 1114112 | tf_op jit(solution)/shard_map/all_gather | solution.py:15
  84.1 108.6 %all-gather.21.cloned.1.call-start = ((), (), s32[]{:S(2)}) async-start(), calls=%async_computation.4 | async-start | bytes 1114112 | tf_op jit(solution)/shard_map/all_gather | solution.py:15
  146.0 108.4 %all-gather.23.cloned.1.call-start = ((), (), s32[]{:S(2)}) async-start(), calls=%async_computation.5 | async-start | bytes 1114112 | tf_op jit(solution)/shard_map/all_gather | solution.py:15
  207.7 163.5 %all-reduce.4.cloned.1.call-start = ((), (), s32[]{:S(2)}) async-start(), calls=%async_computation | async-start | bytes 131072 | tf_op jit(solution)/shard_map/psum | solution.py:32
  258.7 13.3 %collective-permute-start = (f32[1,4,4096]{2,1,0:T(4,128)S(1)}, f32[1,4,4096]{2,1,0:T(4,128)S(1)}, u32[]{:S(2)}, u32[]{:S(2)}) collective-permute-start(f32[1,4,4096]{2,1,0:T(4,128)S(1)} %get-tuple-element.372), channel_id=1, source_target_pairs={{8,0},{9,1},{10,2},{11,3},{12,4},{13,5},{14,6},{15,7},{24,16},{25,... | collective-permute-start | bytes 196616 | tf_op jit(solution)/shard_map/ppermute | solution.py:27
  272.7 6.1 collective-permute-start.1
  278.9 6.5 collective-permute-start.2
  283.0 136.6 %all-gather.25.cloned.1.call-start = ((), (), s32[]{:S(2)}) async-start(), calls=%async_computation.6 | async-start | bytes 1114112 | tf_op jit(solution)/shard_map/all_gather | solution.py:15
  285.4 85.8 %collective-permute-start.3 = (f32[1,4,4096]{2,1,0:T(4,128)S(1)}, f32[1,4,4096]{2,1,0:T(4,128)S(1)}, u32[]{:S(2)}, u32[]{:S(2)}) collective-permute-start(f32[1,4,4096]{2,1,0:T(4,128)S(1)} %broadcast_select_fusion.7), channel_id=1, source_target_pairs={{1,0},{2,1},{3,2},{4,3},{5,4},{6,5},{7,6},{8,7},{9,8},{10,9},{11,1... | collective-permute-start | bytes 196616 | tf_op jit(solution)/shard_map/ppermute | solution.py:27
  383.5 97.7 %all-gather.27.cloned.1.call-start = ((), (), s32[]{:S(2)}) async-start(), calls=%async_computation.7 | async-start | bytes 1114112 | tf_op jit(solution)/shard_map/all_gather | solution.py:15
  434.5 108.5 %all-gather.29.cloned.1.call-start = ((), (), s32[]{:S(2)}) async-start(), calls=%async_computation.8 | async-start | bytes 1114112 | tf_op jit(solution)/shard_map/all_gather | solution.py:15
  496.4 108.3 %all-gather.31.cloned.1.call-start = ((), (), s32[]{:S(2)}) async-start(), calls=%async_computation.9 | async-start | bytes 1114112 | tf_op jit(solution)/shard_map/all_gather | solution.py:15
  558.0 164.2 %all-reduce.6.cloned.1.call-start = ((), (), s32[]{:S(2)}) async-start(), calls=%async_computation.1 | async-start | bytes 131072 | tf_op jit(solution)/shard_map/psum | solution.py:32
  609.0 13.3 %collective-permute-start.4 = (f32[1,4,4096]{2,1,0:T(4,128)S(1)}, f32[1,4,4096]{2,1,0:T(4,128)S(1)}, u32[]{:S(2)}, u32[]{:S(2)}) collective-permute-start(f32[1,4,4096]{2,1,0:T(4,128)S(1)} %get-tuple-element.373), channel_id=1, source_target_pairs={{8,0},{9,1},{10,2},{11,3},{12,4},{13,5},{14,6},{15,7},{24,16},{25,... | collective-permute-start | bytes 196616 | tf_op jit(solution)/shard_map/ppermute | solution.py:27
  623.0 6.1 collective-permute-start.5
  629.2 6.5 collective-permute-start.6
  635.7 86.5 %collective-permute-start.7 = (f32[1,4,4096]{2,1,0:T(4,128)S(1)}, f32[1,4,4096]{2,1,0:T(4,128)S(1)}, u32[]{:S(2)}, u32[]{:S(2)}) collective-permute-start(f32[1,4,4096]{2,1,0:T(4,128)S(1)} %broadcast_select_fusion.4), channel_id=1, source_target_pairs={{1,0},{2,1},{3,2},{4,3},{5,4},{6,5},{7,6},{8,7},{9,8},{10,9},{11,1... | collective-permute-start | bytes 196616 | tf_op jit(solution)/shard_map/ppermute | solution.py:27
Sparse Core Ops, SparseCore 0:
  31.0 37.9 all-gather.16
  84.2 46.5 all-gather.18
  146.1 46.5 all-gather.20
  207.8 46.5 all-gather.22
  283.1 88.0 all-reduce.3
  383.6 35.8 all-gather.24
  434.6 46.5 all-gather.26
  496.5 46.4 all-gather.28
  558.1 46.5 all-gather.30
  633.4 88.7 all-reduce.5
where the time goes:
time: 744 us; the launch traced here: 731 us
  waiting for transfers between devices  542 us (73%)
  matrix products  92.9 us (12%)
  other arithmetic  37.7 us (5%)
  between operations  33 us (4%)
  starting transfers between devices  20.5 us (3%)
    all_gather x8, waiting for transfers between devices, entering(): gathered = lax.all_gather(part, axis)  354 us
    psum x2, waiting for transfers between devices, from_root(): return lax.psum(block, axis)  162 us
    dot_general x8, matrix products, denoise(): return jnp.dot(out_weight, hidden_two, preferred_element_type=jnp.float32)  65.3 us
    add x32, other arithmetic, add_terms(): return earlier + later  27.8 us
    dot_general x8, matrix products, denoise(): jnp.dot(in_weight, state.astype(jnp.bfloat16), preferred_element_type=jnp...  26.4 us
    ppermute x8, waiting for transfers between devices, from_behind(): return lax.ppermute(value, axis, pairs)  26.4 us
    ppermute x8, starting transfers between devices, from_behind(): return lax.ppermute(value, axis, pairs)  20.1 us
  transfers between devices with their start and end apart: 18, of which 16 were waited for; matrix products, arithmetic and copies ran while one was open for 0% of the time, Pallas kernels for 0%

commit v1 on v0

v1 whole, which is shorter than its diff:
```python
import functools
import math

import jax
import jax.numpy as jnp
import numpy as np
from jax import lax
from jax.experimental import pallas as pl
from jax.experimental.pallas import tpu as pltpu
from jax.sharding import PartitionSpec as P

TSTEPS = 1000
ITERS = 4
ROUNDS = 2
LANES = 128
BASE = 32
XROWS = 16
GROUP_MOST = 15


def alpha_table():
    levels = np.arange(TSTEPS, dtype=np.float64)
    low = math.sqrt(0.00085)
    high = math.sqrt(0.012)
    betas = (low + (high - low) * levels / (TSTEPS - 1)) ** 2
    return np.exp(np.cumsum(np.log1p(-betas))).astype(np.float32)


def trig_tables(width):
    half = width // 2
    freqs = np.exp(-math.log(10000.0) * np.arange(half, dtype=np.float64) / half)[:, None]
    digits = np.arange(BASE, dtype=np.float64)[None]
    high, low = freqs * digits * BASE, freqs * digits
    coarse = np.concatenate([np.cos(high), np.sin(high)]).astype(np.float32)
    fine = np.concatenate([np.cos(low), np.sin(low)]).astype(np.float32)
    return coarse, fine


def round_up(value, unit):
    return -(-value // unit) * unit


def kernel(
    n, pix, width, depth, group, direct,
    states_ref, sched_ref, adv_ref, alpha_ref, inw_ref, timew_ref, midw_ref, outw_ref, coarse_ref, fine_ref,
    out_ref, err_ref,
    xin, xs, fin, errs, erecv, lhs, mid, outw, coef_one, coef_two, spread,
    in_send, in_recv, out_send, out_recv, err_send, err_recv,
):
    lat = outw_ref.shape[0]
    ch = midw_ref.shape[0]
    me = lax.axis_index("steps")
    span = ROUNDS * n
    f32, bf16 = jnp.float32, jnp.bfloat16

    def peer(hop):
        return lax.rem(me + hop, n)

    def source(d):
        if direct:
            return states_ref.at[0, :, pl.ds(pl.multiple_of(d * pix, LANES), pix)]
        return states_ref.at[d]

    def target(d):
        if direct:
            return out_ref.at[0, :, pl.ds(pl.multiple_of(d * pix, LANES), pix)]
        return out_ref.at[d]

    def in_copy(d, slot):
        return pltpu.make_async_remote_copy(
            src_ref=source(d), dst_ref=xin.at[slot], send_sem=in_send.at[d], recv_sem=in_recv.at[slot],
            device_id={"steps": d}, device_id_type=pl.DeviceIdType.MESH)

    def out_copy(d, slot):
        return pltpu.make_async_remote_copy(
            src_ref=fin.at[d], dst_ref=target(slot), send_sem=out_send.at[d], recv_sem=out_recv.at[slot],
            device_id={"steps": d}, device_id_type=pl.DeviceIdType.MESH)

    def err_copy(d, slot):
        return pltpu.make_async_remote_copy(
            src_ref=errs.at[d], dst_ref=erecv.at[slot], send_sem=err_send.at[d], recv_sem=err_recv.at[slot],
            device_id={"steps": d}, device_id_type=pl.DeviceIdType.MESH)

    def each_peer(act):
        if n <= 16:
            for hop in range(1, n):
                act(peer(hop))
        else:
            @pl.loop(1, n)
            def _(hop):
                act(peer(hop))

    barrier = pltpu.get_barrier_semaphore()
    each_peer(lambda d: pl.semaphore_signal(
        barrier, inc=1, device_id={"steps": d}, device_id_type=pl.DeviceIdType.MESH))

    lane = lax.broadcasted_iota(jnp.int32, (1, depth), 1) - XROWS
    member = jnp.where((lane >= 0) & (lane < 3 * span), lax.rem(jnp.maximum(lane, 0), span), -1)
    advance_one = adv_ref[0]

    def coefficients(m, stamps):
        place = jnp.where(m >= n, advance_one + m - n, m)
        now, after = sched_ref[place], sched_ref[place + 1]
        a_now = jnp.full((8, LANES), alpha_ref[now], f32)
        a_after = jnp.full((8, LANES), alpha_ref[after], f32)
        one = jnp.sqrt(a_after / a_now)
        two = jnp.sqrt(1.0 - a_after) - one * jnp.sqrt(1.0 - a_now)
        coef_one[m] = one - 1.0
        coef_two[m] = two
        return jnp.where(member == m, now, stamps)

    stamps = lax.fori_loop(0, span, coefficients, jnp.zeros((1, depth), jnp.int32), unroll=4)

    pl.semaphore_wait(barrier, n - 1)
    each_peer(lambda d: in_copy(d, me).start())

    digit = lax.broadcasted_iota(jnp.int32, (BASE, depth), 0)
    hot_high = (digit == lax.shift_right_logical(stamps, 5)).astype(f32)
    hot_low = (digit == lax.bitwise_and(stamps, BASE - 1)).astype(f32)
    exact = lax.Precision.HIGHEST
    high = jnp.dot(coarse_ref[...], hot_high, precision=exact, preferred_element_type=f32)
    low = jnp.dot(fine_ref[...], hot_low, precision=exact, preferred_element_type=f32)
    half = ch // 2
    cos_h, sin_h, cos_l, sin_l = high[:half], high[half:], low[:half], low[half:]
    feats = jnp.concatenate([cos_h * cos_l - sin_h * sin_l, sin_h * cos_l + cos_h * sin_l], axis=0)
    embed = 0.5 * jnp.dot(timew_ref[...], feats, precision=exact, preferred_element_type=f32)
    spread[...] = jnp.zeros_like(spread)
    spread[:, 0:lat] = inw_ref[...].astype(f32) * 0.5
    top = embed.astype(bf16).astype(f32)
    rest = embed - top
    middle = rest.astype(bf16).astype(f32)
    bottom = (rest - middle).astype(bf16).astype(f32)
    part = jnp.where(lane < span, top, jnp.where(lane < 2 * span, middle, bottom))
    part = jnp.where(member >= 0, part, 0.0)
    lhs[...] = (spread[...] + part).astype(bf16)
    mid[...] = (midw_ref[...].astype(f32) * 0.5).astype(bf16)
    outw[...] = jnp.zeros_like(outw)
    outw[0:lat, :] = outw_ref[...].astype(f32)

    xs[...] = jnp.zeros_like(xs)
    if direct:
        xs[me, 0:lat, :] = states_ref[0, :, pl.ds(pl.multiple_of(me * pix, LANES), pix)]
    else:
        xs[me, 0:lat, :] = states_ref[me]

    def arrived(d):
        in_copy(d, d).wait_recv()
        xs[d, 0:lat, :] = xin[d]

    each_peer(arrived)

    hot_row = lax.broadcasted_iota(jnp.int32, (depth - XROWS, LANES), 0)
    hot_member = jnp.where(hot_row < 3 * span, lax.rem(hot_row, span), -1)
    outs = outw[...].astype(bf16)
    wide = lambda tile: jnp.concatenate([tile] * (width // LANES), axis=1) if width > LANES else tile

    def first(x, m):
        hot = wide((hot_member == m).astype(f32).astype(bf16))
        padded = jnp.concatenate([x, jnp.zeros((XROWS - 8, width), f32)], axis=0).astype(bf16)
        pre = jnp.dot(lhs[...], jnp.concatenate([padded, hot], axis=0), preferred_element_type=f32)
        return pre, (pre + pre * jnp.tanh(pre)).astype(bf16)

    def second(pre, hidden):
        mixed = jnp.dot(mid[...], hidden, preferred_element_type=f32)
        return (mixed * (1.0 + jnp.tanh(mixed)) + (pre + pre)).astype(bf16)

    def third(hidden):
        return jnp.dot(outs, hidden, preferred_element_type=f32)

    def note_error(row, k, change):
        square = change * change
        if pix < width:
            square = jnp.where(lax.broadcasted_iota(jnp.int32, square.shape, 1) < pix, square, 0.0)
        total = square[:, 0:LANES]
        for start in range(LANES, width, LANES):
            total = total + square[:, start:start + LANES]
        errs[k, pl.ds(row, 1), :] = jnp.sum(total, axis=0, keepdims=True)

    def one_round(r, carry):
        def sweep(i, carry):
            row = r * ITERS + i

            def some(g, running):
                ks = [g * group + j for j in range(group)]
                olds = [xs[k] for k in ks]
                ones = [None] * group
                twos = [None] * group
                noises = [None] * group
                for step in range(group + 2):
                    if step < group:
                        ones[step] = first(olds[step], r * n + ks[step])
                    if 0 <= step - 1 < group:
                        twos[step - 1] = second(*ones[step - 1])
                    if 0 <= step - 2 < group:
                        noises[step - 2] = third(twos[step - 2])
                for j, k in enumerate(ks):
                    m = r * n + k
                    note_error(row, k, running - olds[j])
                    xs[k] = running
                    running = running + (wide(coef_one[m]) * olds[j] + wide(coef_two[m]) * noises[j])
                return running

            running = lax.fori_loop(0, (n - 1) // group, some, xs[0])
            note_error(row, n - 1, running - xs[n - 1])
            xs[n - 1] = running
            return carry

        lax.fori_loop(0, ITERS, sweep, 0)
        advance = adv_ref[r]

        def shift(k, carry):
            xs[k] = xs[jnp.minimum(k + advance, n - 1)]
            return carry

        lax.fori_loop(0, n, shift, 0, unroll=4)
        return carry

    lax.fori_loop(0, ROUNDS, one_round, 0)
    for k in range(n):
        fin[k] = xs[k, 0:lat, :]
    each_peer(lambda d: out_copy(d, me).start())
    each_peer(lambda d: err_copy(d, me).start())
    if direct:
        out_ref[0, :, pl.ds(pl.multiple_of(me * pix, LANES), pix)] = fin[me]
    else:
        out_ref[me] = fin[me]
    erecv[me] = errs[me]
    each_peer(lambda d: err_copy(d, d).wait_recv())
    sums = lax.fori_loop(0, n, lambda k, total: total + erecv[k], jnp.zeros((ROUNDS * ITERS, LANES), f32), unroll=4)
    err_ref[...] = jnp.sum(sums, axis=1, keepdims=True) * (1.0 / (lat * n * pix))
    each_peer(lambda d: out_copy(d, d).wait_recv())
    each_peer(lambda d: in_copy(d, me).wait_send())
    each_peer(lambda d: out_copy(d, me).wait_send())
    each_peer(lambda d: err_copy(d, me).wait_send())


def shards(states, t_sched, advances, in_weight, time_weight, mid_weight, out_weight):
    n = lax.axis_size("steps")
    _, lat, rows = states.shape
    ch = mid_weight.shape[0]
    pix = rows // n
    direct = pix % LANES == 0
    width = round_up(pix, LANES)
    depth = round_up(XROWS + 3 * ROUNDS * n, LANES)
    group = max(g for g in range(1, GROUP_MOST + 1) if (n - 1) % g == 0)
    coarse, fine = trig_tables(time_weight.shape[1])
    if direct:
        sent = states
        out_shape = states.shape
    else:
        sent = jnp.pad(states.reshape(lat, n, pix).transpose(1, 0, 2), ((0, 0), (0, 0), (0, width - pix)))
        out_shape = sent.shape
    vmem = pl.BlockSpec(memory_space=pltpu.VMEM)
    smem = pl.BlockSpec(memory_space=pltpu.SMEM)
    f32, bf16 = jnp.float32, jnp.bfloat16
    final, errors = pl.pallas_call(
        functools.partial(kernel, n, pix, width, depth, group, direct),
        out_shape=(jax.ShapeDtypeStruct(out_shape, f32), jax.ShapeDtypeStruct((ROUNDS * ITERS, 1), f32)),
        in_specs=[vmem, smem, smem, smem, vmem, vmem, vmem, vmem, vmem, vmem],
        out_specs=(vmem, vmem),
        scratch_shapes=[
            pltpu.VMEM((n, lat, width), f32),
            pltpu.VMEM((n, 8, width), f32),
            pltpu.VMEM((n, lat, width), f32),
            pltpu.VMEM((n, ROUNDS * ITERS, LANES), f32),
            pltpu.VMEM((n, ROUNDS * ITERS, LANES), f32),
            pltpu.VMEM((ch, depth), bf16),
            pltpu.VMEM((ch, ch), bf16),
            pltpu.VMEM((8, ch), f32),
            pltpu.VMEM((ROUNDS * n, 8, LANES), f32),
            pltpu.VMEM((ROUNDS * n, 8, LANES), f32),
            pltpu.VMEM((ch, depth), f32),
        ] + [pltpu.SemaphoreType.DMA((n,))] * 6,
        compiler_params=pltpu.CompilerParams(
            collective_id=0, has_side_effects=True, vmem_limit_bytes=48 * 1024 * 1024),
        name="picard",
    )(sent, t_sched, advances, jnp.asarray(alpha_table()), in_weight, time_weight, mid_weight, out_weight,
      jnp.asarray(coarse), jnp.asarray(fine))
    if not direct:
        final = final[:, :, :pix].transpose(1, 0, 2).reshape(states.shape)
    return final, errors.reshape(ROUNDS, ITERS, 1)


def solution(mesh):
    in_specs = (P(("groups", "steps"), None, None), P("groups"), P("groups"), P(), P(), P(), P())
    out_specs = (P(("groups", "steps"), None, None), P("groups", None, "steps"))
    return jax.shard_map(shards, mesh=mesh, in_specs=in_specs, out_specs=out_specs, check_vma=False)
```

time: 744 us -> 50.5 us (0.07)
  the two profiles are of different devices: /device:TPU:10 before, /device:TPU:0 now
where the time goes in v1:
time: 50.5 us; the launch traced here: 50.3 us
  Pallas kernels  43.5 us (86%)
  local copies, waits for them, and re-layouts  5.97 us (12%)
  between operations  0.73 us (1%)
    pallas_call x1, Pallas kernels, shards(): pl.pallas_call(functools.partial(kernel, n, pix, width, depth, group, dir...  43.5 us
    unnamed x20, local copies, waits for them, and re-layouts  5.32 us

profile of v1, /device:TPU:0, one launch (start us, length us, event | category | flops | bytes accessed | tf_op | source)
XLA Modules:
  0.0 50.3 jit_solution(3961063906719010759)
XLA Ops:
  0.6 0.0 copy-start.5
  0.6 0.0 copy-start.6
  0.7 0.0 copy-start.8
  0.7 0.0 copy-start.7
  0.7 0.0 copy-start.4
  0.7 0.9 %copy.14.inw_ref = bf16[320,4]{1,0:T(8,128)(2,1)S(1)} copy(bf16[320,4]{0,1:T(4,128)(2,1)} %param.13) | data formatting | bytes 5120 | tf_op args[3]
  1.6 0.0 copy-done.5
  1.6 0.0 copy-done.6
  1.6 0.0 copy-done.8
  1.6 0.0 copy-done.7
  1.6 0.0 copy-done.4
  1.6 0.0 copy-start
  1.6 1.0 %copy-done = f32[320,320]{1,0:T(8,128)S(1)} copy-done((f32[320,320]{1,0:T(8,128)S(1)}, f32[320,320]{1,0:T(8,128)}, u32[]{:S(2)}) %copy-start) | copy-done | bytes 409624
  2.6 0.0 copy-start.1
  2.6 0.9 %copy-done.1 = bf16[320,320]{1,0:T(8,128)(2,1)S(1)} copy-done((bf16[320,320]{1,0:T(8,128)(2,1)S(1)}, bf16[320,320]{1,0:T(8,128)(2,1)}, u32[]{:S(2)}) %copy-start.1) | copy-done | bytes 204824
  3.6 0.0 copy-start.2
  3.6 0.9 %copy-done.2 = f32[320,32]{1,0:T(8,128)S(1)} copy-done((f32[320,32]{1,0:T(8,128)S(1)}, f32[320,32]{1,0:T(8,128)}, u32[]{:S(2)}) %copy-start.2) | copy-done | bytes 40984
  4.5 0.0 copy-start.3
  4.5 0.9 %copy-done.3 = f32[320,32]{1,0:T(8,128)S(1)} copy-done((f32[320,32]{1,0:T(8,128)S(1)}, f32[320,32]{1,0:T(8,128)}, u32[]{:S(2)}) %copy-start.3) | copy-done | bytes 40984
  5.4 43.5 %picard.1 = (f32[1,4,4096]{2,1,0:T(4,128)S(1)}, f32[8,1]{1,0:T(8,128)S(1)}) custom-call(f32[1,4,4096]{2,1,0:T(4,128)S(1)} %copy-done.4, s32[33]{0:T(128)S(1)} %copy-done.7, s32[2]{0:T(128)S(1)} %copy-done.8, f32[1000]{0:T(1024)S(1)} %copy-done.5, bf16[320,4]{1,0:T(8,128)(2,1)S(1)} %copy.14.inw_ref, f32[320,320]{1,0:T(8,128)S(1)} %copy-done, ...), custom_call_target="tpu_custom_call" | custom-call | tf_op jit(solution)/shard_map/picard/pallas_call | solution.py:256
  48.9 0.1 reduce
  49.0 0.6 %reshape.7 = f32[2,4,1]{1,0,2:T(2,128)} reshape(f32[8]{0:T(128)S(1)} %reduce) | data formatting | bytes 64 | tf_op jit(solution)/shard_map/reshape | solution.py:281
  49.6 0.6 %copy.17 = f32[1,4,4096]{2,1,0:T(4,128)} copy(f32[1,4,4096]{2,1,0:T(4,128)S(1)} %get-tuple-element.12) | data formatting | bytes 131072
Async XLA Ops:
  0.6 0.9 %copy-start.5 = (f32[1000]{0:T(1024)S(1)}, f32[1000]{0:T(1024)}, u32[]{:S(2)}) copy-start(f32[1000]{0:T(1024)} %constant.6.clone.alpha_ref) | copy-start | bytes 12004
  0.6 0.9 %copy-start.6 = (bf16[4,320]{1,0:T(4,128)(2,1)S(1)}, bf16[4,320]{1,0:T(4,128)(2,1)}, u32[]{:S(2)}) copy-start(bf16[4,320]{1,0:T(4,128)(2,1)} %outw_ref.1) | copy-start | bytes 7684
  0.7 0.9 %copy-start.8 = (s32[2]{0:T(128)S(1)}, s32[2]{0:T(128)}, u32[]{:S(2)}) copy-start(s32[2]{0:T(128)} %adv_ref.1) | copy-start | bytes 28
  0.7 0.9 %copy-start.7 = (s32[33]{0:T(128)S(1)}, s32[33]{0:T(128)}, u32[]{:S(2)}) copy-start(s32[33]{0:T(128)} %sched_ref.1) | copy-start | bytes 400
  0.7 0.9 %copy-start.4 = (f32[1,4,4096]{2,1,0:T(4,128)S(1)}, f32[1,4,4096]{2,1,0:T(4,128)}, u32[]{:S(2)}) copy-start(f32[1,4,4096]{2,1,0:T(4,128)} %states_ref.1) | copy-start | bytes 196612
  1.6 1.0 %copy-start = (f32[320,320]{1,0:T(8,128)S(1)}, f32[320,320]{1,0:T(8,128)}, u32[]{:S(2)}) copy-start(f32[320,320]{1,0:T(8,128)} %timew_ref.1) | copy-start | bytes 1228804
  2.6 0.9 %copy-start.1 = (bf16[320,320]{1,0:T(8,128)(2,1)S(1)}, bf16[320,320]{1,0:T(8,128)(2,1)}, u32[]{:S(2)}) copy-start(bf16[320,320]{1,0:T(8,128)(2,1)} %midw_ref.1) | copy-start | bytes 614404
  3.6 0.9 %copy-start.2 = (f32[320,32]{1,0:T(8,128)S(1)}, f32[320,32]{1,0:T(8,128)}, u32[]{:S(2)}) copy-start(f32[320,32]{1,0:T(8,128)} %constant.8.clone.fine_ref) | copy-start | bytes 122884
  4.5 0.9 %copy-start.3 = (f32[320,32]{1,0:T(8,128)S(1)}, f32[320,32]{1,0:T(8,128)}, u32[]{:S(2)}) copy-start(f32[320,32]{1,0:T(8,128)} %constant.7.clone.coarse_ref) | copy-start | bytes 122884

commit v2 on v1

--- a/solution.py
+++ b/solution.py
@@ -33,7 +33,7 @@
     high, low = freqs * digits * BASE, freqs * digits
     coarse = np.concatenate([np.cos(high), np.sin(high)]).astype(np.float32)
     fine = np.concatenate([np.cos(low), np.sin(low)]).astype(np.float32)
-    return coarse, fine
+    return np.concatenate([coarse, fine])
 
 
 def round_up(value, unit):
@@ -42,13 +42,13 @@
 
 def kernel(
     n, pix, width, depth, group, direct,
-    states_ref, sched_ref, adv_ref, alpha_ref, inw_ref, timew_ref, midw_ref, outw_ref, coarse_ref, fine_ref,
+    states_hbm, sched_ref, adv_ref, alpha_ref, inw_hbm, outw_hbm, timew_hbm, midw_hbm, trig_hbm,
     out_ref, err_ref,
-    xin, xs, fin, errs, erecv, lhs, mid, outw, coef_one, coef_two, spread,
-    in_send, in_recv, out_send, out_recv, err_send, err_recv,
+    states_ref, inw_ref, outw_ref, timew, midw, trig, xin, xs, fin, errs, elines, erecv, lhs, mid, outw, inw, coef_one, coef_two,
+    local, in_send, in_recv, out_send, out_recv, err_send, err_recv,
 ):
     lat = outw_ref.shape[0]
-    ch = midw_ref.shape[0]
+    ch = midw.shape[0]
     me = lax.axis_index("steps")
     span = ROUNDS * n
     f32, bf16 = jnp.float32, jnp.bfloat16
@@ -78,7 +78,7 @@
 
     def err_copy(d, slot):
         return pltpu.make_async_remote_copy(
-            src_ref=errs.at[d], dst_ref=erecv.at[slot], send_sem=err_send.at[d], recv_sem=err_recv.at[slot],
+            src_ref=elines.at[d], dst_ref=erecv.at[slot], send_sem=err_send.at[d], recv_sem=err_recv.at[slot],
             device_id={"steps": d}, device_id_type=pl.DeviceIdType.MESH)
 
     def each_peer(act):
@@ -90,6 +90,14 @@
             def _(hop):
                 act(peer(hop))
 
+    loads = [
+        pltpu.make_async_copy(source_ref, held, local.at[j])
+        for j, (source_ref, held) in enumerate((
+            (states_hbm, states_ref), (trig_hbm, trig), (timew_hbm, timew), (midw_hbm, midw),
+            (inw_hbm, inw_ref), (outw_hbm, outw_ref)))
+    ]
+    for load in loads:
+        load.start()
     barrier = pltpu.get_barrier_semaphore()
     each_peer(lambda d: pl.semaphore_signal(
         barrier, inc=1, device_id={"steps": d}, device_id_type=pl.DeviceIdType.MESH))
@@ -111,6 +119,7 @@
 
     stamps = lax.fori_loop(0, span, coefficients, jnp.zeros((1, depth), jnp.int32), unroll=4)
 
+    loads[0].wait()
     pl.semaphore_wait(barrier, n - 1)
     each_peer(lambda d: in_copy(d, me).start())
 
@@ -118,24 +127,37 @@
     hot_high = (digit == lax.shift_right_logical(stamps, 5)).astype(f32)
     hot_low = (digit == lax.bitwise_and(stamps, BASE - 1)).astype(f32)
     exact = lax.Precision.HIGHEST
-    high = jnp.dot(coarse_ref[...], hot_high, precision=exact, preferred_element_type=f32)
-    low = jnp.dot(fine_ref[...], hot_low, precision=exact, preferred_element_type=f32)
+    for load in loads[1:]:
+        load.wait()
+    high = jnp.dot(trig[0:ch], hot_high, precision=exact, preferred_element_type=f32)
+    low = jnp.dot(trig[ch:], hot_low, precision=exact, preferred_element_type=f32)
     half = ch // 2
     cos_h, sin_h, cos_l, sin_l = high[:half], high[half:], low[:half], low[half:]
     feats = jnp.concatenate([cos_h * cos_l - sin_h * sin_l, sin_h * cos_l + cos_h * sin_l], axis=0)
-    embed = 0.5 * jnp.dot(timew_ref[...], feats, precision=exact, preferred_element_type=f32)
-    spread[...] = jnp.zeros_like(spread)
-    spread[:, 0:lat] = inw_ref[...].astype(f32) * 0.5
+    embed = 0.5 * jnp.dot(timew[...], feats, precision=exact, preferred_element_type=f32)
+    inw[...] = jnp.zeros_like(inw)
+    inw[0:lat, :] = inw_ref[...].astype(f32) * 0.5
+    unit = (lax.broadcasted_iota(jnp.int32, (8, depth), 0) == lane + XROWS).astype(f32)
+    spread = lax.dot_general(
+        inw[...], unit, (((0,), (0,)), ((), ())), precision=exact, preferred_element_type=f32)
     top = embed.astype(bf16).astype(f32)
     rest = embed - top
     middle = rest.astype(bf16).astype(f32)
     bottom = (rest - middle).astype(bf16).astype(f32)
     part = jnp.where(lane < span, top, jnp.where(lane < 2 * span, middle, bottom))
     part = jnp.where(member >= 0, part, 0.0)
-    lhs[...] = (spread[...] + part).astype(bf16)
-    mid[...] = (midw_ref[...].astype(f32) * 0.5).astype(bf16)
+    left = spread + part
+    lhs[0:ch, :] = left.astype(bf16)
+    mid[...] = (midw[...].astype(f32) * 0.5).astype(bf16)
     outw[...] = jnp.zeros_like(outw)
     outw[0:lat, :] = outw_ref[...].astype(f32)
+    linear = 2.0 * jnp.dot(outw[...], left, precision=exact, preferred_element_type=f32)
+    linear_top = linear.astype(bf16).astype(f32)
+    linear_rest = linear - linear_top
+    linear_middle = linear_rest.astype(bf16).astype(f32)
+    linear_bottom = linear_rest - linear_middle
+    lhs[ch:ch + 32, :] = jnp.concatenate(
+        [linear_top, linear_middle, linear_bottom, jnp.zeros_like(linear)], axis=0).astype(bf16)
 
     xs[...] = jnp.zeros_like(xs)
     if direct:
@@ -157,15 +179,17 @@
     def first(x, m):
         hot = wide((hot_member == m).astype(f32).astype(bf16))
         padded = jnp.concatenate([x, jnp.zeros((XROWS - 8, width), f32)], axis=0).astype(bf16)
-        pre = jnp.dot(lhs[...], jnp.concatenate([padded, hot], axis=0), preferred_element_type=f32)
-        return pre, (pre + pre * jnp.tanh(pre)).astype(bf16)
-
-    def second(pre, hidden):
+        both = jnp.dot(lhs[...], jnp.concatenate([padded, hot], axis=0), preferred_element_type=f32)
+        pre = both[0:ch]
+        tail = both[ch:ch + 8] + both[ch + 8:ch + 16] + both[ch + 16:ch + 24]
+        return tail, (pre + pre * jnp.tanh(pre)).astype(bf16)
+
+    def second(tail, hidden):
         mixed = jnp.dot(mid[...], hidden, preferred_element_type=f32)
-        return (mixed * (1.0 + jnp.tanh(mixed)) + (pre + pre)).astype(bf16)
-
-    def third(hidden):
-        return jnp.dot(outs, hidden, preferred_element_type=f32)
+        return tail, (mixed + mixed * jnp.tanh(mixed)).astype(bf16)
+
+    def third(tail, hidden):
+        return tail + jnp.dot(outs, hidden, preferred_element_type=f32)
 
     def note_error(row, k, change):
         square = change * change
@@ -192,7 +216,7 @@
                     if 0 <= step - 1 < group:
                         twos[step - 1] = second(*ones[step - 1])
                     if 0 <= step - 2 < group:
-                        noises[step - 2] = third(twos[step - 2])
+                        noises[step - 2] = third(*twos[step - 2])
                 for j, k in enumerate(ks):
                     m = r * n + k
                     note_error(row, k, running - olds[j])
@@ -219,15 +243,22 @@
     for k in range(n):
         fin[k] = xs[k, 0:lat, :]
     each_peer(lambda d: out_copy(d, me).start())
+    cells = (ROUNDS * ITERS, LANES)
+    diagonal = lax.broadcasted_iota(jnp.int32, cells, 0) == lax.broadcasted_iota(jnp.int32, cells, 1)
+    for k in range(n):
+        total = jnp.sum(errs[k], axis=1, keepdims=True)
+        elines[k] = jnp.sum(jnp.where(diagonal, total, 0.0), axis=0, keepdims=True)
     each_peer(lambda d: err_copy(d, me).start())
     if direct:
         out_ref[0, :, pl.ds(pl.multiple_of(me * pix, LANES), pix)] = fin[me]
     else:
         out_ref[me] = fin[me]
-    erecv[me] = errs[me]
+    erecv[me] = elines[me]
     each_peer(lambda d: err_copy(d, d).wait_recv())
-    sums = lax.fori_loop(0, n, lambda k, total: total + erecv[k], jnp.zeros((ROUNDS * ITERS, LANES), f32), unroll=4)
-    err_ref[...] = jnp.sum(sums, axis=1, keepdims=True) * (1.0 / (lat * n * pix))
+    sums = lax.fori_loop(0, n, lambda k, total: total + erecv[k], jnp.zeros((1, LANES), f32), unroll=4)
+    means = jnp.sum(jnp.where(diagonal, sums, 0.0), axis=1, keepdims=True) * (1.0 / (lat * n * pix))
+    for r in range(ROUNDS):
+        err_ref[r] = means[r * ITERS:(r + 1) * ITERS]
     each_peer(lambda d: out_copy(d, d).wait_recv())
     each_peer(lambda d: in_copy(d, me).wait_send())
     each_peer(lambda d: out_copy(d, me).wait_send())
@@ -243,7 +274,6 @@
     width = round_up(pix, LANES)
     depth = round_up(XROWS + 3 * ROUNDS * n, LANES)
     group = max(g for g in range(1, GROUP_MOST + 1) if (n - 1) % g == 0)
-    coarse, fine = trig_tables(time_weight.shape[1])
     if direct:
         sent = states
         out_shape = states.shape
@@ -252,33 +282,42 @@
         out_shape = sent.shape
     vmem = pl.BlockSpec(memory_space=pltpu.VMEM)
     smem = pl.BlockSpec(memory_space=pltpu.SMEM)
+    hbm = pl.BlockSpec(memory_space=pltpu.HBM)
     f32, bf16 = jnp.float32, jnp.bfloat16
     final, errors = pl.pallas_call(
         functools.partial(kernel, n, pix, width, depth, group, direct),
-        out_shape=(jax.ShapeDtypeStruct(out_shape, f32), jax.ShapeDtypeStruct((ROUNDS * ITERS, 1), f32)),
-        in_specs=[vmem, smem, smem, smem, vmem, vmem, vmem, vmem, vmem, vmem],
+        out_shape=(jax.ShapeDtypeStruct(out_shape, f32), jax.ShapeDtypeStruct((ROUNDS, ITERS, 1), f32)),
+        in_specs=[hbm, smem, smem, smem, hbm, hbm, hbm, hbm, hbm],
         out_specs=(vmem, vmem),
         scratch_shapes=[
+            pltpu.VMEM(sent.shape, f32),
+            pltpu.VMEM((lat, ch), bf16),
+            pltpu.VMEM((lat, ch), bf16),
+            pltpu.VMEM((ch, ch), f32),
+            pltpu.VMEM((ch, ch), bf16),
+            pltpu.VMEM((2 * ch, BASE), f32),
             pltpu.VMEM((n, lat, width), f32),
             pltpu.VMEM((n, 8, width), f32),
             pltpu.VMEM((n, lat, width), f32),
             pltpu.VMEM((n, ROUNDS * ITERS, LANES), f32),
-            pltpu.VMEM((n, ROUNDS * ITERS, LANES), f32),
-            pltpu.VMEM((ch, depth), bf16),
+            pltpu.VMEM((n, 1, LANES), f32),
+            pltpu.VMEM((n, 1, LANES), f32),
+            pltpu.VMEM((ch + 32, depth), bf16),
             pltpu.VMEM((ch, ch), bf16),
+            pltpu.VMEM((8, ch), f32),
             pltpu.VMEM((8, ch), f32),
             pltpu.VMEM((ROUNDS * n, 8, LANES), f32),
             pltpu.VMEM((ROUNDS * n, 8, LANES), f32),
-            pltpu.VMEM((ch, depth), f32),
+            pltpu.SemaphoreType.DMA((6,)),
         ] + [pltpu.SemaphoreType.DMA((n,))] * 6,
         compiler_params=pltpu.CompilerParams(
-            collective_id=0, has_side_effects=True, vmem_limit_bytes=48 * 1024 * 1024),
+            collective_id=0, has_side_effects=True, vmem_limit_bytes=67043328),
         name="picard",
-    )(sent, t_sched, advances, jnp.asarray(alpha_table()), in_weight, time_weight, mid_weight, out_weight,
-      jnp.asarray(coarse), jnp.asarray(fine))
+    )(sent, t_sched, advances, jnp.asarray(alpha_table()), in_weight.T, out_weight, time_weight, mid_weight,
+      jnp.asarray(trig_tables(time_weight.shape[1])))
     if not direct:
         final = final[:, :, :pix].transpose(1, 0, 2).reshape(states.shape)
-    return final, errors.reshape(ROUNDS, ITERS, 1)
+    return final, errors
 
 
 def solution(mesh):

time: 50.5 us -> 45 us (0.89)
  local copies, waits for them, and re-layouts: 5.97 us -> 2.8 us
  Pallas kernels: 43.5 us -> 41.3 us
    unnamed x20 -> x1, local copies, waits for them, and re-layouts: 5.32 us -> 1.47 us
    pallas_call x1, Pallas kernels: 43.5 us -> 41.3 us  [shards(): pl.pallas_call(functools.partial(kernel, n, pix, width, depth, group, dir...]
    pallas_call x0 -> x1, local copies, waits for them, and re-layouts: none -> 1.33 us  [shards(): pl.pallas_call(functools.partial(kernel, n, pix, width, depth, group, dir...]
    reshape x1 -> x0, local copies, waits for them, and re-layouts: 0.65 us -> none  [shards(): return (final, errors.reshape(ROUNDS, ITERS, 1))]
where the time goes in v2:
time: 45 us; the launch traced here: 44.8 us
  Pallas kernels  41.3 us (92%)
  local copies, waits for them, and re-layouts  2.8 us (6%)
  between operations  0.64 us (1%)
    pallas_call x1, Pallas kernels, shards(): pl.pallas_call(functools.partial(kernel, n, pix, width, depth, group, dir...  41.3 us
    unnamed x1, local copies, waits for them, and re-layouts  1.47 us
    pallas_call x1, local copies, waits for them, and re-layouts, shards(): pl.pallas_call(functools.partial(kernel, n, pix, width, depth, group, dir...  1.33 us

profile of v2, /device:TPU:0, one launch (start us, length us, event | category | flops | bytes accessed | tf_op | source)
XLA Modules:
  0.0 44.8 jit_solution(9597833517982717063)
XLA Ops:
  0.6 41.3 %picard.1 = (f32[1,4,4096]{2,1,0:T(4,128)}, f32[2,4,1]{2,1,0:T(4,128)}) custom-call(f32[1,4,4096]{2,1,0:T(4,128)} %states_hbm.1, s32[33]{0:T(128)} %sched_ref.1, s32[2]{0:T(128)} %adv_ref.1, f32[1000]{0:T(1024)} %constant.4.clone.alpha_ref, bf16[4,320]{1,0:T(4,128)(2,1)} %bitcast.1, bf16[4,320]{1,0:T(4,128)(2,1)} %outw_hbm.1, f32[320,320]{1,0:T(8,128)} %timew_hbm.1, ...), custom_call_target="tpu_custom_call" | custom-call | tf_op jit(solution)/shard_map/picard/pallas_call | solution.py:287
  42.0 1.3 %copy.11 = f32[2,4,1]{1,2,0:T(1,128)} copy(f32[2,4,1]{2,1,0:T(4,128)} %get-tuple-element.3) | data formatting | bytes 64 | tf_op jit(solution)/shard_map/picard/pallas_call | solution.py:287
  43.3 1.5 %copy.13 = f32[1,4,4096]{2,1,0:T(4,128)} copy(f32[1,4,4096]{2,1,0:T(4,128)} %get-tuple-element.6) | data formatting | bytes 131072

commit v3 on v2

--- a/solution.py
+++ b/solution.py
@@ -41,7 +41,7 @@
 
 
 def kernel(
-    n, pix, width, depth, group, direct,
+    n, pix, width, depth, direct,
     states_hbm, sched_ref, adv_ref, alpha_ref, inw_hbm, outw_hbm, timew_hbm, midw_hbm, trig_hbm,
     out_ref, err_ref,
     states_ref, inw_ref, outw_ref, timew, midw, trig, xin, xs, fin, errs, elines, erecv, lhs, mid, outw, inw, coef_one, coef_two,
@@ -160,6 +160,7 @@
         [linear_top, linear_middle, linear_bottom, jnp.zeros_like(linear)], axis=0).astype(bf16)
 
     xs[...] = jnp.zeros_like(xs)
+    errs[...] = jnp.zeros_like(errs)
     if direct:
         xs[me, 0:lat, :] = states_ref[0, :, pl.ds(pl.multiple_of(me * pix, LANES), pix)]
     else:
@@ -201,35 +202,34 @@
         errs[k, pl.ds(row, 1), :] = jnp.sum(total, axis=0, keepdims=True)
 
     def one_round(r, carry):
-        def sweep(i, carry):
+        def some(row, ks, running):
+            count = len(ks)
+            olds = [xs[k] for k in ks]
+            ones = [None] * count
+            twos = [None] * count
+            noises = [None] * count
+            for step in range(count + 2):
+                if step < count:
+                    ones[step] = first(olds[step], r * n + ks[step])
+                if 0 <= step - 1 < count:
+                    twos[step - 1] = second(*ones[step - 1])
+                if 0 <= step - 2 < count:
+                    noises[step - 2] = third(*twos[step - 2])
+            for j, k in enumerate(ks):
+                m = r * n + k
+                note_error(row, k, running - olds[j])
+                xs[k] = running
+                running = running + (wide(coef_one[m]) * olds[j] + wide(coef_two[m]) * noises[j])
+            return running
+
+        for i in range(ITERS):
             row = r * ITERS + i
-
-            def some(g, running):
-                ks = [g * group + j for j in range(group)]
-                olds = [xs[k] for k in ks]
-                ones = [None] * group
-                twos = [None] * group
-                noises = [None] * group
-                for step in range(group + 2):
-                    if step < group:
-                        ones[step] = first(olds[step], r * n + ks[step])
-                    if 0 <= step - 1 < group:
-                        twos[step - 1] = second(*ones[step - 1])
-                    if 0 <= step - 2 < group:
-                        noises[step - 2] = third(*twos[step - 2])
-                for j, k in enumerate(ks):
-                    m = r * n + k
-                    note_error(row, k, running - olds[j])
-                    xs[k] = running
-                    running = running + (wide(coef_one[m]) * olds[j] + wide(coef_two[m]) * noises[j])
-                return running
-
-            running = lax.fori_loop(0, (n - 1) // group, some, xs[0])
+            if n <= GROUP_MOST + 1:
+                running = some(row, list(range(i, n - 1)), xs[i])
+            else:
+                running = lax.fori_loop(i, n - 1, lambda k, held: some(row, [k], held), xs[i])
             note_error(row, n - 1, running - xs[n - 1])
             xs[n - 1] = running
-            return carry
-
-        lax.fori_loop(0, ITERS, sweep, 0)
         advance = adv_ref[r]
 
         def shift(k, carry):
@@ -273,7 +273,6 @@
     direct = pix % LANES == 0
     width = round_up(pix, LANES)
     depth = round_up(XROWS + 3 * ROUNDS * n, LANES)
-    group = max(g for g in range(1, GROUP_MOST + 1) if (n - 1) % g == 0)
     if direct:
         sent = states
         out_shape = states.shape
@@ -285,7 +284,7 @@
     hbm = pl.BlockSpec(memory_space=pltpu.HBM)
     f32, bf16 = jnp.float32, jnp.bfloat16
     final, errors = pl.pallas_call(
-        functools.partial(kernel, n, pix, width, depth, group, direct),
+        functools.partial(kernel, n, pix, width, depth, direct),
         out_shape=(jax.ShapeDtypeStruct(out_shape, f32), jax.ShapeDtypeStruct((ROUNDS, ITERS, 1), f32)),
         in_specs=[hbm, smem, smem, smem, hbm, hbm, hbm, hbm, hbm],
         out_specs=(vmem, vmem),

time: 45 us -> 41.6 us (0.924)
  Pallas kernels: 41.3 us -> 37.9 us
    pallas_call x1, Pallas kernels: 41.3 us -> 37.9 us  [shards(): pl.pallas_call(functools.partial(kernel, n, pix, width, depth, direct), o...]
where the time goes in v3:
time: 41.6 us; the launch traced here: 41.4 us
  Pallas kernels  37.9 us (91%)
  local copies, waits for them, and re-layouts  2.8 us (7%)
  between operations  0.64 us (2%)
    pallas_call x1, Pallas kernels, shards(): pl.pallas_call(functools.partial(kernel, n, pix, width, depth, direct), o...  37.9 us
    unnamed x1, local copies, waits for them, and re-layouts  1.47 us
    pallas_call x1, local copies, waits for them, and re-layouts, shards(): pl.pallas_call(functools.partial(kernel, n, pix, width, depth, direct), o...  1.33 us

profile of v3, /device:TPU:0, one launch (start us, length us, event | category | flops | bytes accessed | tf_op | source)
XLA Modules:
  0.0 41.4 jit_solution(1174170519360940201)
XLA Ops:
  0.6 37.9 %picard.1 = (f32[1,4,4096]{2,1,0:T(4,128)}, f32[2,4,1]{2,1,0:T(4,128)}) custom-call(f32[1,4,4096]{2,1,0:T(4,128)} %states_hbm.1, s32[33]{0:T(128)} %sched_ref.1, s32[2]{0:T(128)} %adv_ref.1, f32[1000]{0:T(1024)} %constant.4.clone.alpha_ref, bf16[4,320]{1,0:T(4,128)(2,1)} %bitcast.1, bf16[4,320]{1,0:T(4,128)(2,1)} %outw_hbm.1, f32[320,320]{1,0:T(8,128)} %timew_hbm.1, ...), custom_call_target="tpu_custom_call" | custom-call | tf_op jit(solution)/shard_map/picard/pallas_call | solution.py:286
  38.6 1.3 %copy.11 = f32[2,4,1]{1,2,0:T(1,128)} copy(f32[2,4,1]{2,1,0:T(4,128)} %get-tuple-element.3) | data formatting | bytes 64 | tf_op jit(solution)/shard_map/picard/pallas_call | solution.py:286
  39.9 1.5 %copy.13 = f32[1,4,4096]{2,1,0:T(4,128)} copy(f32[1,4,4096]{2,1,0:T(4,128)} %get-tuple-element.6) | data formatting | bytes 131072
